TPU v7x, 32 devices: a whole 2x2x4 slice. The times are simulated.
32 devices in a mesh: modes: 8 (over z, y), cheb: 4 (over x, core).
Axes of the slice: x: 2, y: 2, z: 4, core: 2. Of those that a mesh axis runs over, the one named last changes fastest.
Arguments:
- start: float32 [2, 2, 2048, 256], P(None, None, ('modes', 'cheb')), may hold values from -45 to 45
- forcing: float32 [2, 2, 2048, 256], P(None, None, ('modes', 'cheb')), may hold values from -45 to 45
- taus: float32 [2048, 256, 256], P(('modes', 'cheb')), may hold values from -5 to 5
Outputs:
- solution: float32 [2, 2, 2048, 256], P(None, None, ('modes', 'cheb'))
All inputs are finite; a program needn't handle non-finite values.
Results may differ from a plain program's by a relative error of at most 0.0002.
Values sent between devices are 32-bit elements; how exact they have to be, the bound alone decides.
A program may use at most 128 MiB of HBM per device.

v0:
```python
import functools
import math

import jax
import jax.numpy as jnp
import numpy as np
from jax import lax
from jax.experimental import pallas as pl
from jax.experimental.pallas import tpu as pltpu
from jax.sharding import PartitionSpec as P

NEWTON = 2
KRYLOV = 3


PREC = lax.Precision.HIGH
STRENGTH = 0.1
AXES = ("modes", "cheb")
STAT_LANES = 128
LANES = 128


def cheb_rows(degree_count):
    degree = jnp.arange(degree_count, dtype=jnp.int32)[:, None]
    node = 2 * jnp.arange(degree_count, dtype=jnp.int32)[None, :] + 1
    turns = degree * node % (4 * degree_count)
    return jnp.cos(2.0 * math.pi / (4 * degree_count) * turns.astype(jnp.float32))


def phase_table(row_count, col_count, period):
    row_index = jnp.arange(row_count, dtype=jnp.int32)[:, None]
    col_index = jnp.arange(col_count, dtype=jnp.int32)[None, :]
    turns = row_index * col_index % period
    angle = 2.0 * math.pi / period * turns.astype(jnp.float32)
    return (jnp.cos(angle), jnp.sin(angle))


def least_squares(hessen, beta_norm):
    steps_count = len(hessen)
    matrix = [
        [hessen[col_index][:, row_index] for row_index in range(col_index + 2)]
        for col_index in range(steps_count)
    ]
    target = [beta_norm] + [jnp.zeros_like(beta_norm) for row_index in range(steps_count)]
    cosines = []
    sines_list = []
    for col_index in range(steps_count):
        column = matrix[col_index]
        for row_index in range(col_index):
            upper_entry = (
                cosines[row_index] * column[row_index]
                + sines_list[row_index] * column[row_index + 1]
            )
            lower_entry = (
                cosines[row_index] * column[row_index + 1]
                - sines_list[row_index] * column[row_index]
            )
            column[row_index] = upper_entry
            column[row_index + 1] = lower_entry
        radius = jnp.sqrt(
            column[col_index] * column[col_index] + column[col_index + 1] * column[col_index + 1]
        )
        cosines.append(column[col_index] / radius)
        sines_list.append(column[col_index + 1] / radius)
        column[col_index] = radius
        target[col_index + 1] = -sines_list[col_index] * target[col_index]
        target[col_index] = cosines[col_index] * target[col_index]
    solved = [None] * steps_count
    for row_index in reversed(range(steps_count)):
        partial_sum = target[row_index]
        for col_index in range(row_index + 1, steps_count):
            partial_sum = partial_sum - matrix[col_index][row_index] * solved[col_index]
        solved[row_index] = partial_sum / matrix[row_index][row_index]
    return solved


def shards(start, forcing, taus):
    group_size = lax.axis_size(AXES)
    batch, parts, local_modes, degrees = start.shape
    total_modes = local_modes * group_size
    points_count = 2 * total_modes
    outer_len = max(2 ** ((points_count.bit_length() - 1) // 2), local_modes)
    inner_len = points_count // outer_len
    half_inner = inner_len // 2
    split = outer_len // local_modes
    rows = degrees // group_size
    block_lanes = batch * 2 * local_modes
    fields = rows * batch
    spread = 1.0 / math.sqrt(total_modes * degrees)
    gather_factor = math.sqrt(total_modes * degrees) / points_count
    cheb_table = cheb_rows(degrees)
    tau_keep = (jnp.arange(degrees) < degrees - 2).astype(jnp.float32)
    coef_weights = jnp.where(jnp.arange(degrees) == 0, 1.0, 2.0).astype(jnp.float32) / degrees
    back_table = cheb_table * (coef_weights * tau_keep)[:, None]

    section_cos, section_sin = phase_table(inner_len, half_inner, inner_len)
    value_table = jnp.stack([section_cos, section_sin])
    slope_table = jnp.stack([-section_sin, section_cos])
    back_cos, back_sin = section_cos.T, section_sin.T
    twist_cos, twist_sin = phase_table(inner_len, outer_len, points_count)
    final_cos, final_sin = phase_table(outer_len, outer_len, outer_len)
    turn_cos = (
        twist_cos[:, :, None] * final_cos[None] - twist_sin[:, :, None] * final_sin[None]
    )
    turn_sin = (
        twist_sin[:, :, None] * final_cos[None] + twist_cos[:, :, None] * final_sin[None]
    )
    turn_table = lax.optimization_barrier(
        jnp.concatenate([turn_cos, -turn_sin, -turn_sin, -turn_cos], axis=1)
    )
    mode = (
        outer_len * jnp.arange(half_inner, dtype=jnp.int32)[:, None]
        + jnp.arange(outer_len, dtype=jnp.int32)[None, :]
    )
    paired_mode = jnp.concatenate([mode, mode], axis=1)[:, None, :]
    weights = jnp.where(paired_mode == 0, 1.0, 2.0).astype(jnp.float32) * spread
    slope_weights = weights * (16.0 * paired_mode.astype(jnp.float32) / total_modes)

    def exchange(blocks):
        return lax.all_to_all(blocks, AXES, split_axis=0, concat_axis=0, tiled=True)

    def stat_block(stats):
        flat = jnp.pad(stats.reshape(-1), (0, STAT_LANES - stats.size))
        return jnp.broadcast_to(flat, (group_size, rows, STAT_LANES))

    def read_stats(received, shape):
        flat = jnp.sum(received[:, 0, :], axis=0)
        return flat[: math.prod(shape)].reshape(shape)

    def to_points(coefs, stats):
        values = jnp.einsum("ni,brkn->ibrk", cheb_table, coefs, precision=PREC)
        blocks = values.reshape(group_size, rows, block_lanes)
        if stats is not None:
            blocks = jnp.concatenate([blocks, stat_block(stats)], axis=2)
        received = exchange(blocks)
        summed = None
        if stats is not None:
            summed = read_stats(received[:, :, block_lanes:], stats.shape)
            received = received[:, :, :block_lanes]
        spectrum = received.reshape(half_inner, split, rows, batch, 2, local_modes)
        spectrum = spectrum.transpose(0, 2, 3, 4, 1, 5).reshape(
            half_inner, fields, 2 * outer_len
        )

        def points_of(table, weighted):
            turned = jnp.einsum("sjq,qyl->jysl", table, weighted, precision=PREC)
            turned = turned.reshape(inner_len, fields, 4 * outer_len)
            return jnp.einsum("jyl,jlt->jyt", turned, turn_table, precision=PREC)

        values = points_of(value_table, spectrum * weights)
        slopes = points_of(slope_table, spectrum * slope_weights)
        return (values, slopes), summed

    def to_coefficients(points):
        turned = jnp.einsum("jyt,jlt->jyl", points, turn_table, precision=PREC) * gather_factor
        direct = turned[:, :, : 2 * outer_len].reshape(inner_len, -1)
        swapped = turned[:, :, 2 * outer_len :].reshape(inner_len, -1)
        spectrum = jnp.dot(back_cos, direct, precision=PREC) + jnp.dot(
            back_sin, swapped, precision=PREC
        )
        blocks = spectrum.reshape(half_inner, rows, batch, 2, split, local_modes)
        blocks = blocks.transpose(0, 4, 1, 2, 3, 5).reshape(group_size, rows, block_lanes)
        received = exchange(blocks).reshape(degrees, batch, 2, local_modes)
        return jnp.einsum("ibrk,ni->brkn", received, back_table, precision=PREC)

    def precondition(coefs):
        return jnp.einsum("kam,brkm->brka", taus, coefs, precision=PREC)

    def on_points(scale):
        return jnp.tile(scale, rows)[None, :, None]

    def on_coefs(scale):
        return scale[:, None, None, None]

    iterate = start
    kept_forcing = forcing * tau_keep
    base, nothing = to_points(iterate, None)
    for newton_step in range(NEWTON):
        base_points, base_slopes = base
        residual = iterate + precondition(
            to_coefficients(STRENGTH * base_points * base_slopes) - kept_forcing
        )
        local_square = jnp.sum(residual * residual, axis=(1, 2, 3))
        image, squared = to_points(residual, local_square)
        beta_norm = jnp.sqrt(squared)
        krylov_basis = [-residual / on_coefs(beta_norm)]
        images = [tuple(-part / on_points(beta_norm) for part in image)]
        hessen = []
        for column in range(KRYLOV):
            probe_points, probe_slopes = images[column]
            product = STRENGTH * (base_points * probe_slopes + probe_points * base_slopes)
            applied = krylov_basis[column] + precondition(to_coefficients(product))
            local_stats = jnp.stack(
                [jnp.sum(vector * applied, axis=(1, 2, 3)) for vector in krylov_basis + [applied]],
                axis=1,
            )
            last = column == KRYLOV - 1
            if last:
                stats = read_stats(exchange(stat_block(local_stats)), local_stats.shape)
            else:
                image, stats = to_points(applied, local_stats)
            projections, square = stats[:, :-1], stats[:, -1]
            length = jnp.sqrt(square - jnp.sum(projections * projections, axis=1))
            hessen.append(jnp.concatenate([projections, length[:, None]], axis=1))
            if not last:
                for index in range(column + 1):
                    applied = applied - on_coefs(projections[:, index]) * krylov_basis[index]
                    image = tuple(
                        part - on_points(projections[:, index]) * known
                        for part, known in zip(image, images[index])
                    )
                krylov_basis.append(applied / on_coefs(length))
                images.append(tuple(part / on_points(length) for part in image))
        solved = least_squares(hessen, beta_norm)
        for column in range(KRYLOV):
            iterate = iterate + on_coefs(solved[column]) * krylov_basis[column]
            base = tuple(
                part + on_points(solved[column]) * known
                for part, known in zip(base, images[column])
            )
    return iterate


def split_table(table):
    table = np.asarray(table, np.float32)
    high = table.astype(jnp.bfloat16)
    low = (table - high.astype(np.float32)).astype(jnp.bfloat16)
    return high, low


def left_table(table):
    high, low = split_table(table)
    return np.concatenate([high, low, high], axis=1)


def tables_of(local_modes, group_size, degrees):
    total = local_modes * group_size
    points = 2 * total
    inner = points // local_modes
    half = local_modes // 2
    spread = 1.0 / math.sqrt(total * degrees)
    degree = np.arange(degrees)[:, None]
    node = 2 * np.arange(degrees)[None, :] + 1
    cheb = np.cos(2.0 * np.pi / (4 * degrees) * (degree * node % (4 * degrees)))
    coef_weights = np.where(np.arange(degrees) == 0, 1.0, 2.0) / degrees
    keep = np.arange(degrees) < degrees - 2
    to_rows = left_table(cheb.T)
    to_degrees = left_table(cheb * (coef_weights * keep)[:, None])

    j_low = np.arange(inner)[:, None]
    source = np.arange(group_size)[None, :]
    angle = 2.0 * np.pi / inner * (j_low * source % inner)
    cos, sin = np.cos(angle), np.sin(angle)
    real = np.concatenate([cos, -sin], axis=1)
    imag = np.concatenate([sin, cos], axis=1)
    wave = np.tile(16.0 * local_modes * source / total, (1, 2))
    gather = 2.0 * spread * np.concatenate([real, imag, real * wave, imag * wave], axis=0)
    gather = left_table(gather)
    scatter = np.concatenate(
        [np.concatenate([cos.T, sin.T], axis=1), np.concatenate([-sin.T, cos.T], axis=1)], axis=0
    )
    scatter = left_table(scatter * math.sqrt(total * degrees) / points)

    lane_mode = np.tile(np.arange(local_modes), 2)[None, :]
    twist = 2.0 * np.pi / points * (j_low * lane_mode)
    wave_low = np.broadcast_to(16.0 * lane_mode / total, twist.shape)
    twist = np.stack([np.cos(twist), np.sin(twist), wave_low]).astype(np.float32)

    mode = np.arange(local_modes)
    final = 2.0 * np.pi / local_modes * (mode[:, None] * mode[None, :] % local_modes)
    pair = np.eye(2)
    cos_high, cos_low = split_table(np.kron(pair, np.cos(final)))
    sin_high, sin_low = split_table(np.kron(pair, np.sin(final)))
    cos_row = np.concatenate([cos_high, cos_low], axis=1)
    sin_row = np.concatenate([-sin_high, -sin_low], axis=1)
    finish = np.concatenate([cos_row, sin_row, cos_row, sin_row], axis=0)
    high_row = np.concatenate([cos_high, -sin_high], axis=1)
    low_row = np.concatenate([cos_low, -sin_low], axis=1)
    begin = np.concatenate([high_row, high_row, low_row], axis=0)
    return to_rows, to_degrees, gather, scatter, twist, finish, begin


def split(value):
    high = value.astype(jnp.bfloat16)
    return high, (value - high.astype(jnp.float32)).astype(jnp.bfloat16)


def right_operand(value):
    high, low = split(value)
    return jnp.concatenate([high, high, low], axis=0)


def dot(left, right):
    return jnp.dot(left, right, preferred_element_type=jnp.float32)


def flow_solver(
    sizes,
    start_ref,
    forcing_ref,
    taus_ref,
    to_rows_ref,
    to_degrees_ref,
    gather_ref,
    scatter_ref,
    twist_ref,
    finish_ref,
    begin_ref,
    out_ref,
    tau_terms,
    stage,
    vectors,
    applied,
    right,
    images,
    image,
    out_fwd,
    in_fwd,
    out_back,
    in_back,
    out_stat,
    in_stat,
    history,
    stage_sem,
    fwd_send,
    fwd_recv,
    back_send,
    back_recv,
    stat_send,
    stat_recv,
):
    group_size, minor, local_modes, rows, degrees, inner = sizes
    half = local_modes // 2
    me = lax.axis_index(AXES[0]) * minor + lax.axis_index(AXES[1])
    lane = lax.broadcasted_iota(jnp.int32, (1, LANES), 1)
    first_half = lane % local_modes < half
    low_flow = lane < local_modes

    def own_rows(index):
        return pl.ds(pl.multiple_of(index * rows, rows), rows)

    def exchange(src, dst, send_sem, recv_sem):
        def step(offset, carry):
            peer = lax.rem(me + offset, group_size)
            pltpu.make_async_remote_copy(
                src_ref=src.at[:, own_rows(peer), :],
                dst_ref=dst.at[:, own_rows(me), :],
                send_sem=send_sem,
                recv_sem=recv_sem,
                device_id=(peer // minor, lax.rem(peer, minor)),
                device_id_type=pl.DeviceIdType.MESH,
            ).start()
            return carry

        pltpu.make_async_copy(
            src.at[:, own_rows(me), :], dst.at[:, own_rows(me), :], recv_sem
        ).start()
        lax.fori_loop(1, group_size, step, 0)

    def finish_exchange(src, dst, send_sem, recv_sem):
        sent = pl.ds(0, (group_size - 1) * rows)
        pltpu.make_async_copy(src.at[:, sent, :], dst.at[:, sent, :], send_sem).wait()
        pltpu.make_async_copy(src, dst, recv_sem).wait()

    def to_modes(first, second):
        turned = pltpu.roll(second, half, 1)
        back = pltpu.roll(first, LANES - half, 1)
        return jnp.where(first_half, first, turned), jnp.where(first_half, back, second)

    def send_values(first, second):
        operand = right_operand(jnp.concatenate([first, second], axis=1))
        values = dot(to_rows_ref[...], operand)
        wide = lax.broadcasted_iota(jnp.int32, (1, 2 * LANES), 1)
        constant = jnp.logical_and(me == 0, wide % half == 0)
        constant = jnp.logical_and(constant, wide < LANES)
        values = values * jnp.where(constant, 0.5, 1.0)
        out_fwd[0] = values[:, :LANES]
        out_fwd[1] = values[:, LANES:]
        exchange(out_fwd, in_fwd, fwd_send, fwd_recv)

    def points_of_rows(pair):
        columns = []
        for row in (2 * pair, 2 * pair + 1):
            picked = pl.ds(row, group_size, stride=rows)
            real, imag = to_modes(in_fwd[0, picked, :], in_fwd[1, picked, :])
            columns.append(jnp.concatenate([real, imag], axis=0))
        operand = right_operand(jnp.concatenate(columns, axis=1))
        summed = dot(gather_ref[...], operand)
        cos, sin, low = twist_ref[0], twist_ref[1], twist_ref[2]
        lefts = []
        for index in range(2):
            part = summed[:, index * LANES : (index + 1) * LANES]
            real, imag, wave_real, wave_imag = (
                part[n * inner : (n + 1) * inner] for n in range(4)
            )
            slope_real = -(wave_imag + low * imag)
            slope_imag = wave_real + low * real
            for re, im in ((real, imag), (slope_real, slope_imag)):
                re_high, re_low = split(re * cos - im * sin)
                im_high, im_low = split(re * sin + im * cos)
                lefts.append(jnp.concatenate([re_high, im_high, re_low, im_low], axis=1))
        wide = dot(jnp.concatenate(lefts, axis=0), finish_ref[...])
        points = wide[:, :LANES] + wide[:, LANES:]
        for index in range(2):
            where = pl.ds((2 * pair + index) * inner, inner)
            image[0, where, :] = points[2 * index * inner : (2 * index + 1) * inner]
            image[1, where, :] = points[(2 * index + 1) * inner : (2 * index + 2) * inner]

    def receive_points():
        finish_exchange(out_fwd, in_fwd, fwd_send, fwd_recv)
        for pair in range(rows // 2):
            points_of_rows(pair)

    def modes_of_rows(pair, slot, factor):
        where = pl.ds(2 * pair * inner, 2 * inner)
        product = factor * (
            images[0, 0, where, :] * images[slot, 1, where, :]
            + images[slot, 0, where, :] * images[0, 1, where, :]
        )
        high, low = split(product)
        turned = dot(jnp.concatenate([high, low, high], axis=1), begin_ref[...])
        cos, sin = twist_ref[0], twist_ref[1]
        columns = []
        for index in range(2):
            part = turned[index * inner : (index + 1) * inner]
            real, imag = part[:, :LANES], part[:, LANES:]
            columns.append(
                jnp.concatenate([real * cos + imag * sin, imag * cos - real * sin], axis=0)
            )
        operand = right_operand(jnp.concatenate(columns, axis=1))
        summed = dot(scatter_ref[...], operand)
        for index in range(2):
            part = summed[:, index * LANES : (index + 1) * LANES]
            first, second = to_modes(part[:group_size], part[group_size:])
            picked = pl.ds(2 * pair + index, group_size, stride=rows)
            out_back[0, picked, :] = first
            out_back[1, picked, :] = second

    def precondition():
        per_step = 8
        for side in range(2):
            operand = right[side]

            def step(block, carry):
                base = side * half + block * per_step
                where = pl.ds(pl.multiple_of(base * degrees, degrees), per_step * degrees)
                wide = dot(tau_terms[where, :], operand)
                narrow = wide[:, :LANES] + wide[:, LANES:]
                total = applied[side]
                for index in range(per_step):
                    mine = lane % half == block * per_step + index
                    total = jnp.where(mine, narrow[index * degrees : (index + 1) * degrees], total)
                applied[side] = total
                return carry

            lax.fori_loop(0, half // per_step, step, 0)

    def by_flow(values, masks):
        low = jnp.sum(jnp.where(jnp.logical_and(masks, low_flow), values, 0.0), axis=1, keepdims=True)
        high = jnp.sum(
            jnp.where(jnp.logical_and(masks, ~low_flow), values, 0.0), axis=1, keepdims=True
        )
        return jnp.where(low_flow, low, high)

    stat_row = lax.broadcasted_iota(jnp.int32, (8, LANES), 0)
    stat_lane = lax.broadcasted_iota(jnp.int32, (8, LANES), 1) % local_modes
    packed = stat_row == stat_lane

    def send_stats(partial):
        sums = by_flow(partial, stat_row >= 0)
        out_stat[...] = jnp.sum(jnp.where(packed, sums, 0.0), axis=0, keepdims=True)

        def step(offset, carry):
            peer = lax.rem(me + offset, group_size)
            pltpu.make_async_remote_copy(
                src_ref=out_stat,
                dst_ref=in_stat.at[me],
                send_sem=stat_send,
                recv_sem=stat_recv,
                device_id=(peer // minor, lax.rem(peer, minor)),
                device_id_type=pl.DeviceIdType.MESH,
            ).start()
            return carry

        pltpu.make_async_copy(out_stat, in_stat.at[me], stat_recv).start()
        lax.fori_loop(1, group_size, step, 0)

    def receive_stats():
        sent = pl.ds(0, group_size - 1)
        pltpu.make_async_copy(in_stat.at[sent], in_stat.at[sent], stat_send).wait()
        pltpu.make_async_copy(in_stat, in_stat, stat_recv).wait()
        total = jnp.sum(in_stat[...], axis=0)
        return by_flow(jnp.broadcast_to(total, (8, LANES)), packed)

    vectors[...] = jnp.zeros_like(vectors)
    images[...] = jnp.zeros_like(images)
    vectors[0] = start_ref[...]
    send_values(start_ref[0], start_ref[1])

    chunk = stage.shape[1]
    chunks = tau_terms.shape[0] // chunk

    def fetch(index, slot):
        where = pl.ds(pl.multiple_of(index * chunk, chunk), chunk)
        return pltpu.make_async_copy(taus_ref.at[where, :], stage.at[slot], stage_sem.at[slot])

    fetch(0, 0).start()

    def load(index, carry):
        slot = lax.rem(index, 2)

        @pl.when(index + 1 < chunks)
        def _():
            fetch(index + 1, 1 - slot).start()

        fetch(index, slot).wait()
        high, low = split(stage[slot])
        where = pl.ds(pl.multiple_of(index * chunk, chunk), chunk)
        tau_terms[where, :degrees] = high
        tau_terms[where, degrees:] = low
        return carry

    lax.fori_loop(0, chunks, load, 0)

    receive_points()
    images[0] = image[...]

    def iteration(index, carry):
        phase = lax.rem(index, KRYLOV + 1)
        opening = phase == 0
        factor = jnp.where(opening, 0.5 * STRENGTH, STRENGTH)
        for pair in range(rows // 2):
            modes_of_rows(pair, phase, factor)
        exchange(out_back, in_back, back_send, back_recv)
        finish_exchange(out_back, in_back, back_send, back_recv)
        operand = right_operand(jnp.concatenate([in_back[0], in_back[1]], axis=1))
        coefs = dot(to_degrees_ref[...], operand)
        drive = jnp.where(opening, 1.0, 0.0)
        for side in range(2):
            part = coefs[:, side * LANES : (side + 1) * LANES] - drive * forcing_ref[side]
            high, low = split(part)
            both = jnp.concatenate([high, low], axis=1)
            right[side, :degrees] = both
            right[side, degrees:] = both
        precondition()
        partial = [jnp.zeros((1, LANES), jnp.float32) for _ in range(4)]
        for side in range(2):
            whole = vectors[phase, side] + applied[side]
            applied[side] = whole
            for known in range(KRYLOV):
                partial[known] += jnp.sum(vectors[known + 1, side] * whole, axis=0, keepdims=True)
            partial[KRYLOV] += jnp.sum(whole * whole, axis=0, keepdims=True)
        used = [jnp.where(known < phase, partial[known], 0.0) for known in range(KRYLOV)]
        zero = jnp.zeros((1, LANES), jnp.float32)
        send_stats(jnp.concatenate(used + [partial[KRYLOV]] + [zero] * (7 - KRYLOV), axis=0))

        @pl.when(phase < KRYLOV)
        def _():
            send_values(applied[0], applied[1])

        stats = receive_stats()
        history[phase] = stats
        inner_products = [stats[known : known + 1] for known in range(KRYLOV)]
        square = stats[KRYLOV : KRYLOV + 1]
        for value in inner_products:
            square = square - value * value
        scale = jnp.where(opening, -1.0, 1.0) / jnp.sqrt(square)

        @pl.when(phase < KRYLOV)
        def _():
            for side in range(2):
                whole = applied[side]
                for known in range(KRYLOV):
                    whole = whole - inner_products[known] * vectors[known + 1, side]
                vectors[phase + 1, side] = scale * whole
            receive_points()
            for part in range(2):
                whole = image[part]
                for known in range(KRYLOV):
                    whole = whole - inner_products[known] * images[known + 1, part]
                images[phase + 1, part] = scale * whole

        @pl.when(phase == KRYLOV)
        def _():
            hessen = []
            for column in range(KRYLOV):
                kept = history[column + 1]
                entries = [kept[known : known + 1] for known in range(column + 1)]
                length = kept[KRYLOV : KRYLOV + 1]
                for value in entries:
                    length = length - value * value
                hessen.append(jnp.stack(entries + [jnp.sqrt(length)], axis=1))
            solved = least_squares(hessen, jnp.sqrt(history[0][KRYLOV : KRYLOV + 1]))
            for side in range(2):
                whole = vectors[0, side]
                for known in range(KRYLOV):
                    whole = whole + solved[known] * vectors[known + 1, side]
                vectors[0, side] = whole
            for part in range(2):
                whole = images[0, part]
                for known in range(KRYLOV):
                    whole = whole + solved[known] * images[known + 1, part]
                images[0, part] = whole

        return carry

    lax.fori_loop(0, NEWTON * (KRYLOV + 1), iteration, 0)
    out_ref[...] = vectors[0]


def solve_flows(start, forcing, taus):
    group_size = lax.axis_size(AXES)
    minor = lax.axis_size(AXES[1])
    batch, parts, local_modes, degrees = start.shape
    rows = degrees // group_size
    inner = 2 * group_size
    half = local_modes // 2
    tables = tables_of(local_modes, group_size, degrees)
    sizes = (group_size, minor, local_modes, rows, degrees, inner)

    def pack(field):
        field = field.reshape(batch, parts, 2, half, degrees)
        return field.transpose(2, 4, 0, 1, 3).reshape(2, degrees, LANES)

    def unpack(field):
        field = field.reshape(2, degrees, batch, parts, half)
        return field.transpose(2, 3, 0, 4, 1).reshape(batch, parts, local_modes, degrees)

    field = (2, degrees, LANES)
    image = (2, rows * inner, LANES)
    chunk = 4 * degrees
    vmem = pl.BlockSpec(memory_space=pltpu.VMEM)
    out = pl.pallas_call(
        functools.partial(flow_solver, sizes),
        out_shape=jax.ShapeDtypeStruct(field, jnp.float32),
        in_specs=[vmem, vmem, pl.BlockSpec(memory_space=pl.ANY)] + [vmem] * len(tables),
        out_specs=vmem,
        scratch_shapes=[
            pltpu.VMEM((local_modes * degrees, 2 * degrees), jnp.bfloat16),
            pltpu.VMEM((2, chunk, degrees), jnp.float32),
            pltpu.VMEM((KRYLOV + 1,) + field, jnp.float32),
            pltpu.VMEM(field, jnp.float32),
            pltpu.VMEM((2, 2 * degrees, 2 * LANES), jnp.bfloat16),
            pltpu.VMEM((KRYLOV + 1,) + image, jnp.float32),
            pltpu.VMEM(image, jnp.float32),
            pltpu.VMEM(field, jnp.float32),
            pltpu.VMEM(field, jnp.float32),
            pltpu.VMEM(field, jnp.float32),
            pltpu.VMEM(field, jnp.float32),
            pltpu.VMEM((1, LANES), jnp.float32),
            pltpu.VMEM((group_size, 1, LANES), jnp.float32),
            pltpu.VMEM((KRYLOV + 1, 8, LANES), jnp.float32),
            pltpu.SemaphoreType.DMA((2,)),
        ]
        + [pltpu.SemaphoreType.DMA] * 6,
        compiler_params=pltpu.CompilerParams(
            has_side_effects=True, vmem_limit_bytes=56 * 1024 * 1024
        ),
    )(
        pack(start),
        pack(forcing * (jnp.arange(degrees) < degrees - 2).astype(jnp.float32)),
        taus.reshape(local_modes * degrees, degrees),
        *[jnp.asarray(table) for table in tables],
    )
    return unpack(out)


def fits_kernel(start):
    batch, parts, local_modes, degrees = start.shape
    rows = degrees // lax.axis_size(AXES)
    return (batch, parts, rows, batch * local_modes) == (2, 2, 8, LANES)


def local_step(start, forcing, taus):
    if fits_kernel(start):
        return solve_flows(start, forcing, taus)
    return shards(start, forcing, taus)


def solution(mesh):
    return jax.shard_map(
        local_step,
        mesh=mesh,
        in_specs=(
            P(None, None, ("modes", "cheb"), None),
            P(None, None, ("modes", "cheb"), None),
            P(("modes", "cheb"), None, None),
        ),
        out_specs=P(None, None, ("modes", "cheb"), None),
        check_vma=False,
    )
```

profile of v0, /device:TPU:0, one launch (start us, length us, event | category | flops | bytes accessed | tf_op | source)
XLA Modules:
  0.0 222.6 jit_solution(2227261455272048750)
XLA Ops:
  0.0 1.0 broadcast_multiply_fusion
  1.0 0.8 copy.20.forcing_ref
  1.8 1.0 copy.17
  2.8 0.8 copy.19.start_ref
  3.6 217.1 %shard_map.100 = f32[2,256,128]{2,1,0:T(8,128)} custom-call(f32[2,256,128]{2,1,0:T(8,128)} %copy.19.start_ref, f32[2,256,128]{2,1,0:T(8,128)} %copy.20.forcing_ref, f32[16384,256]{1,0:T(8,128)} %bitcast.13, bf16[256,768]{1,0:T(8,128)(2,1)} %constant.16.clone.to_rows_ref, bf16[256,768]{1,0:T(8,128)(2,1)} %constant.17.clone.to_degrees_ref, ...), custom_call_target="tpu_custom_call" | custom-call | tf_op jit(solution)/shard_map/pallas_call | solution.py:633
  220.8 1.1 copy.21
  221.9 0.7 copy.22
  (2 shorter events, 0.0 us)
where the time goes:
time: 223 us
  Pallas kernels  217 us (97%)
  local copies, waits for them, and re-layouts  4.45 us (2%)
    pallas_call x1, Pallas kernels, solve_flows(): pl.pallas_call(functools.partial(flow_solver, sizes), out_shape=jax.Shape...  217 us

commit v1 on v0

--- a/solution.py
+++ b/solution.py
@@ -233,6 +233,11 @@
     return np.concatenate([high, low, high], axis=1)
 
 
+def right_table(table):
+    high, low = split_table(table)
+    return np.concatenate([high, high, low], axis=0)
+
+
 def tables_of(local_modes, group_size, degrees):
     total = local_modes * group_size
     points = 2 * total
@@ -245,7 +250,7 @@
     coef_weights = np.where(np.arange(degrees) == 0, 1.0, 2.0) / degrees
     keep = np.arange(degrees) < degrees - 2
     to_rows = left_table(cheb.T)
-    to_degrees = left_table(cheb * (coef_weights * keep)[:, None])
+    to_degrees = right_table(cheb * (coef_weights * keep)[:, None])
 
     j_low = np.arange(inner)[:, None]
     source = np.arange(group_size)[None, :]
@@ -311,7 +316,8 @@
     stage,
     vectors,
     applied,
-    right,
+    partial,
+    driven,
     images,
     image,
     out_fwd,
@@ -331,6 +337,7 @@
 ):
     group_size, minor, local_modes, rows, degrees, inner = sizes
     half = local_modes // 2
+    per_dot = 4
     me = lax.axis_index(AXES[0]) * minor + lax.axis_index(AXES[1])
     lane = lax.broadcasted_iota(jnp.int32, (1, LANES), 1)
     first_half = lane % local_modes < half
@@ -339,27 +346,35 @@
     def own_rows(index):
         return pl.ds(pl.multiple_of(index * rows, rows), rows)
 
+    flips = []
+    for bit in range(group_size.bit_length() - 1):
+        flips.append((1 << bit) - (2 << bit) * lax.rem(me // (1 << bit), 2))
+
+    def peers():
+        for distance in reversed(range(1, group_size)):
+            peer = me
+            for bit, flip in enumerate(flips):
+                if distance >> bit & 1:
+                    peer = peer + flip
+            yield peer, (peer // minor, lax.rem(peer, minor))
+
     def exchange(src, dst, send_sem, recv_sem):
-        def step(offset, carry):
-            peer = lax.rem(me + offset, group_size)
+        for peer, place in peers():
             pltpu.make_async_remote_copy(
-                src_ref=src.at[:, own_rows(peer), :],
-                dst_ref=dst.at[:, own_rows(me), :],
+                src_ref=src.at[own_rows(peer), :],
+                dst_ref=dst.at[own_rows(me), :],
                 send_sem=send_sem,
                 recv_sem=recv_sem,
-                device_id=(peer // minor, lax.rem(peer, minor)),
+                device_id=place,
                 device_id_type=pl.DeviceIdType.MESH,
             ).start()
-            return carry
-
         pltpu.make_async_copy(
-            src.at[:, own_rows(me), :], dst.at[:, own_rows(me), :], recv_sem
+            src.at[own_rows(me), :], dst.at[own_rows(me), :], recv_sem
         ).start()
-        lax.fori_loop(1, group_size, step, 0)
 
     def finish_exchange(src, dst, send_sem, recv_sem):
         sent = pl.ds(0, (group_size - 1) * rows)
-        pltpu.make_async_copy(src.at[:, sent, :], dst.at[:, sent, :], send_sem).wait()
+        pltpu.make_async_copy(src.at[sent, :], dst.at[sent, :], send_sem).wait()
         pltpu.make_async_copy(src, dst, recv_sem).wait()
 
     def to_modes(first, second):
@@ -367,16 +382,11 @@
         back = pltpu.roll(first, LANES - half, 1)
         return jnp.where(first_half, first, turned), jnp.where(first_half, back, second)
 
-    def send_values(first, second):
-        operand = right_operand(jnp.concatenate([first, second], axis=1))
-        values = dot(to_rows_ref[...], operand)
-        wide = lax.broadcasted_iota(jnp.int32, (1, 2 * LANES), 1)
-        constant = jnp.logical_and(me == 0, wide % half == 0)
-        constant = jnp.logical_and(constant, wide < LANES)
-        values = values * jnp.where(constant, 0.5, 1.0)
-        out_fwd[0] = values[:, :LANES]
-        out_fwd[1] = values[:, LANES:]
-        exchange(out_fwd, in_fwd, fwd_send, fwd_recv)
+    def send_values(side, field):
+        values = dot(to_rows_ref[...], right_operand(field))
+        constant = jnp.logical_and(me + side == 0, lane % half == 0)
+        out_fwd[side] = values * jnp.where(constant, 0.5, 1.0)
+        exchange(out_fwd.at[side], in_fwd.at[side], fwd_send.at[side], fwd_recv.at[side])
 
     def points_of_rows(pair):
         columns = []
@@ -407,7 +417,10 @@
             image[1, where, :] = points[(2 * index + 1) * inner : (2 * index + 2) * inner]
 
     def receive_points():
-        finish_exchange(out_fwd, in_fwd, fwd_send, fwd_recv)
+        for side in range(2):
+            finish_exchange(
+                out_fwd.at[side], in_fwd.at[side], fwd_send.at[side], fwd_recv.at[side]
+            )
         for pair in range(rows // 2):
             points_of_rows(pair)
 
@@ -436,24 +449,17 @@
             out_back[0, picked, :] = first
             out_back[1, picked, :] = second
 
-    def precondition():
-        per_step = 8
-        for side in range(2):
-            operand = right[side]
-
-            def step(block, carry):
-                base = side * half + block * per_step
-                where = pl.ds(pl.multiple_of(base * degrees, degrees), per_step * degrees)
-                wide = dot(tau_terms[where, :], operand)
-                narrow = wide[:, :LANES] + wide[:, LANES:]
-                total = applied[side]
-                for index in range(per_step):
-                    mine = lane % half == block * per_step + index
-                    total = jnp.where(mine, narrow[index * degrees : (index + 1) * degrees], total)
-                applied[side] = total
-                return carry
-
-            lax.fori_loop(0, half // per_step, step, 0)
+    def precondition(side, operand):
+        for block in range(half // per_dot):
+            base = side * half + block * per_dot
+            where = pl.ds(pl.multiple_of(base * degrees, degrees), per_dot * degrees)
+            wide = dot(tau_terms[where, :], operand)
+            narrow = wide[:, :LANES] + wide[:, LANES:]
+            total = applied[side]
+            for index in range(per_dot):
+                mine = lane % half == block * per_dot + index
+                total = jnp.where(mine, narrow[index * degrees : (index + 1) * degrees], total)
+            applied[side] = total
 
     def by_flow(values, masks):
         low = jnp.sum(jnp.where(jnp.logical_and(masks, low_flow), values, 0.0), axis=1, keepdims=True)
@@ -470,20 +476,16 @@
         sums = by_flow(partial, stat_row >= 0)
         out_stat[...] = jnp.sum(jnp.where(packed, sums, 0.0), axis=0, keepdims=True)
 
-        def step(offset, carry):
-            peer = lax.rem(me + offset, group_size)
+        for peer, place in peers():
             pltpu.make_async_remote_copy(
                 src_ref=out_stat,
                 dst_ref=in_stat.at[me],
                 send_sem=stat_send,
                 recv_sem=stat_recv,
-                device_id=(peer // minor, lax.rem(peer, minor)),
+                device_id=place,
                 device_id_type=pl.DeviceIdType.MESH,
             ).start()
-            return carry
-
         pltpu.make_async_copy(out_stat, in_stat.at[me], stat_recv).start()
-        lax.fori_loop(1, group_size, step, 0)
 
     def receive_stats():
         sent = pl.ds(0, group_size - 1)
@@ -495,7 +497,9 @@
     vectors[...] = jnp.zeros_like(vectors)
     images[...] = jnp.zeros_like(images)
     vectors[0] = start_ref[...]
-    send_values(start_ref[0], start_ref[1])
+    for side in range(2):
+        send_values(side, start_ref[side])
+        driven[side] = dot(to_rows_ref[...], right_operand(forcing_ref[side]))
 
     chunk = stage.shape[1]
     chunks = tau_terms.shape[0] // chunk
@@ -504,8 +508,6 @@
         where = pl.ds(pl.multiple_of(index * chunk, chunk), chunk)
         return pltpu.make_async_copy(taus_ref.at[where, :], stage.at[slot], stage_sem.at[slot])
 
-    fetch(0, 0).start()
-
     def load(index, carry):
         slot = lax.rem(index, 2)
 
@@ -515,12 +517,15 @@
 
         fetch(index, slot).wait()
         high, low = split(stage[slot])
+        combined = dot(jnp.concatenate([high, low, high], axis=1), to_degrees_ref[...])
+        high, low = split(combined)
         where = pl.ds(pl.multiple_of(index * chunk, chunk), chunk)
         tau_terms[where, :degrees] = high
         tau_terms[where, degrees:] = low
         return carry
 
-    lax.fori_loop(0, chunks, load, 0)
+    fetch(0, 0).start()
+    lax.fori_loop(0, chunks // 2, load, 0)
 
     receive_points()
     images[0] = image[...]
@@ -531,33 +536,45 @@
         factor = jnp.where(opening, 0.5 * STRENGTH, STRENGTH)
         for pair in range(rows // 2):
             modes_of_rows(pair, phase, factor)
-        exchange(out_back, in_back, back_send, back_recv)
-        finish_exchange(out_back, in_back, back_send, back_recv)
-        operand = right_operand(jnp.concatenate([in_back[0], in_back[1]], axis=1))
-        coefs = dot(to_degrees_ref[...], operand)
+        for side in range(2):
+            exchange(out_back.at[side], in_back.at[side], back_send.at[side], back_recv.at[side])
+
+        @pl.when(index == 0)
+        def _():
+            lax.fori_loop(chunks // 2, chunks, load, 0)
+
         drive = jnp.where(opening, 1.0, 0.0)
-        for side in range(2):
-            part = coefs[:, side * LANES : (side + 1) * LANES] - drive * forcing_ref[side]
-            high, low = split(part)
+        partial[...] = jnp.zeros_like(partial)
+
+        def half_step(side, carry):
+            finish_exchange(
+                out_back.at[side], in_back.at[side], back_send.at[side], back_recv.at[side]
+            )
+            high, low = split(in_back[side] - drive * driven[side])
             both = jnp.concatenate([high, low], axis=1)
-            right[side, :degrees] = both
-            right[side, degrees:] = both
-        precondition()
-        partial = [jnp.zeros((1, LANES), jnp.float32) for _ in range(4)]
-        for side in range(2):
+            precondition(side, jnp.concatenate([both, both], axis=0))
             whole = vectors[phase, side] + applied[side]
             applied[side] = whole
-            for known in range(KRYLOV):
-                partial[known] += jnp.sum(vectors[known + 1, side] * whole, axis=0, keepdims=True)
-            partial[KRYLOV] += jnp.sum(whole * whole, axis=0, keepdims=True)
-        used = [jnp.where(known < phase, partial[known], 0.0) for known in range(KRYLOV)]
-        zero = jnp.zeros((1, LANES), jnp.float32)
-        send_stats(jnp.concatenate(used + [partial[KRYLOV]] + [zero] * (7 - KRYLOV), axis=0))
-
-        @pl.when(phase < KRYLOV)
-        def _():
-            send_values(applied[0], applied[1])
-
+            sums = [
+                jnp.sum(vectors[known + 1, side] * whole, axis=0, keepdims=True)
+                for known in range(KRYLOV)
+            ]
+            sums = [jnp.where(known < phase, sums[known], 0.0) for known in range(KRYLOV)]
+            sums.append(jnp.sum(whole * whole, axis=0, keepdims=True))
+            sums += [jnp.zeros((1, LANES), jnp.float32)] * (7 - KRYLOV)
+            partial[...] += jnp.concatenate(sums, axis=0)
+
+            @pl.when(side == 1)
+            def _():
+                send_stats(partial[...])
+
+            @pl.when(phase < KRYLOV)
+            def _():
+                send_values(side, applied[side])
+
+            return carry
+
+        lax.fori_loop(0, 2, half_step, 0)
         stats = receive_stats()
         history[phase] = stats
         inner_products = [stats[known : known + 1] for known in range(KRYLOV)]
@@ -640,7 +657,8 @@
             pltpu.VMEM((2, chunk, degrees), jnp.float32),
             pltpu.VMEM((KRYLOV + 1,) + field, jnp.float32),
             pltpu.VMEM(field, jnp.float32),
-            pltpu.VMEM((2, 2 * degrees, 2 * LANES), jnp.bfloat16),
+            pltpu.VMEM((8, LANES), jnp.float32),
+            pltpu.VMEM(field, jnp.float32),
             pltpu.VMEM((KRYLOV + 1,) + image, jnp.float32),
             pltpu.VMEM(image, jnp.float32),
             pltpu.VMEM(field, jnp.float32),
@@ -652,13 +670,14 @@
             pltpu.VMEM((KRYLOV + 1, 8, LANES), jnp.float32),
             pltpu.SemaphoreType.DMA((2,)),
         ]
-        + [pltpu.SemaphoreType.DMA] * 6,
+        + [pltpu.SemaphoreType.DMA((2,))] * 4
+        + [pltpu.SemaphoreType.DMA] * 2,
         compiler_params=pltpu.CompilerParams(
             has_side_effects=True, vmem_limit_bytes=56 * 1024 * 1024
         ),
     )(
         pack(start),
-        pack(forcing * (jnp.arange(degrees) < degrees - 2).astype(jnp.float32)),
+        pack(forcing),
         taus.reshape(local_modes * degrees, degrees),
         *[jnp.asarray(table) for table in tables],
     )
@@ -667,8 +686,10 @@
 
 def fits_kernel(start):
     batch, parts, local_modes, degrees = start.shape
-    rows = degrees // lax.axis_size(AXES)
-    return (batch, parts, rows, batch * local_modes) == (2, 2, 8, LANES)
+    group = lax.axis_size(AXES)
+    rows = degrees // group
+    fits = (batch, parts, rows, batch * local_modes) == (2, 2, 8, LANES)
+    return fits and group & (group - 1) == 0
 
 
 def local_step(start, forcing, taus):

time: 223 us -> 183 us (0.82)
  Pallas kernels: 217 us -> 177 us
    pallas_call x1, Pallas kernels: 217 us -> 177 us  [solve_flows(): pl.pallas_call(functools.partial(flow_solver, sizes), out_shape=jax.Shape...]
where the time goes in v1:
time: 183 us
  Pallas kernels  177 us (97%)
  local copies, waits for them, and re-layouts  5.4 us (3%)
    pallas_call x1, Pallas kernels, solve_flows(): pl.pallas_call(functools.partial(flow_solver, sizes), out_shape=jax.Shape...  177 us

profile of v1, /device:TPU:0, one launch (start us, length us, event | category | flops | bytes accessed | tf_op | source)
XLA Modules:
  0.0 182.5 jit_solution(12463821572624659076)
XLA Ops:
  0.0 1.0 copy.17
  1.0 0.8 copy.19.start_ref
  1.8 1.0 copy.18
  2.8 0.8 copy.20.forcing_ref
  3.6 177.1 %shard_map.100 = f32[2,256,128]{2,1,0:T(8,128)} custom-call(f32[2,256,128]{2,1,0:T(8,128)} %copy.19.start_ref, f32[2,256,128]{2,1,0:T(8,128)} %copy.20.forcing_ref, f32[16384,256]{1,0:T(8,128)} %bitcast.13, bf16[256,768]{1,0:T(8,128)(2,1)} %constant.14.clone.to_rows_ref, bf16[768,256]{1,0:T(8,128)(2,1)} %constant.15.clone.to_degrees_ref, ...), custom_call_target="tpu_custom_call" | custom-call | tf_op jit(solution)/shard_map/pallas_call | solution.py:650
  180.7 1.1 copy.21
  181.8 0.7 copy.22

commit v2 on v1

--- a/solution.py
+++ b/solution.py
@@ -35,12 +35,8 @@
     return (jnp.cos(angle), jnp.sin(angle))
 
 
-def least_squares(hessen, beta_norm):
-    steps_count = len(hessen)
-    matrix = [
-        [hessen[col_index][:, row_index] for row_index in range(col_index + 2)]
-        for col_index in range(steps_count)
-    ]
+def least_squares(matrix, beta_norm):
+    steps_count = len(matrix)
     target = [beta_norm] + [jnp.zeros_like(beta_norm) for row_index in range(steps_count)]
     cosines = []
     sines_list = []
@@ -211,7 +207,10 @@
                     )
                 krylov_basis.append(applied / on_coefs(length))
                 images.append(tuple(part / on_points(length) for part in image))
-        solved = least_squares(hessen, beta_norm)
+        matrix = [
+            [hessen[column][:, row] for row in range(column + 2)] for column in range(KRYLOV)
+        ]
+        solved = least_squares(matrix, beta_norm)
         for column in range(KRYLOV):
             iterate = iterate + on_coefs(solved[column]) * krylov_basis[column]
             base = tuple(
@@ -231,11 +230,6 @@
 def left_table(table):
     high, low = split_table(table)
     return np.concatenate([high, low, high], axis=1)
-
-
-def right_table(table):
-    high, low = split_table(table)
-    return np.concatenate([high, high, low], axis=0)
 
 
 def tables_of(local_modes, group_size, degrees):
@@ -250,7 +244,7 @@
     coef_weights = np.where(np.arange(degrees) == 0, 1.0, 2.0) / degrees
     keep = np.arange(degrees) < degrees - 2
     to_rows = left_table(cheb.T)
-    to_degrees = right_table(cheb * (coef_weights * keep)[:, None])
+    to_degrees = left_table((cheb * (coef_weights * keep)[:, None]).T)
 
     j_low = np.arange(inner)[:, None]
     source = np.arange(group_size)[None, :]
@@ -266,21 +260,23 @@
     )
     scatter = left_table(scatter * math.sqrt(total * degrees) / points)
 
-    lane_mode = np.tile(np.arange(local_modes), 2)[None, :]
+    lane = np.arange(2 * local_modes)
+    lane_mode = (lane // 4 + half * (lane % 2))[None, :]
+    lane_flow = lane // 2 % 2
     twist = 2.0 * np.pi / points * (j_low * lane_mode)
     wave_low = np.broadcast_to(16.0 * lane_mode / total, twist.shape)
     twist = np.stack([np.cos(twist), np.sin(twist), wave_low]).astype(np.float32)
 
-    mode = np.arange(local_modes)
-    final = 2.0 * np.pi / local_modes * (mode[:, None] * mode[None, :] % local_modes)
-    pair = np.eye(2)
-    cos_high, cos_low = split_table(np.kron(pair, np.cos(final)))
-    sin_high, sin_low = split_table(np.kron(pair, np.sin(final)))
+    final = lane_mode.T * np.tile(np.arange(local_modes), 2)[None, :] % local_modes
+    final = 2.0 * np.pi / local_modes * final
+    same = lane_flow[:, None] == lane[None, :] // local_modes
+    cos_high, cos_low = split_table(same * np.cos(final))
+    sin_high, sin_low = split_table(same * np.sin(final))
     cos_row = np.concatenate([cos_high, cos_low], axis=1)
     sin_row = np.concatenate([-sin_high, -sin_low], axis=1)
     finish = np.concatenate([cos_row, sin_row, cos_row, sin_row], axis=0)
-    high_row = np.concatenate([cos_high, -sin_high], axis=1)
-    low_row = np.concatenate([cos_low, -sin_low], axis=1)
+    high_row = np.concatenate([cos_high.T, -sin_high.T], axis=1)
+    low_row = np.concatenate([cos_low.T, -sin_low.T], axis=1)
     begin = np.concatenate([high_row, high_row, low_row], axis=0)
     return to_rows, to_degrees, gather, scatter, twist, finish, begin
 
@@ -297,6 +293,16 @@
 
 def dot(left, right):
     return jnp.dot(left, right, preferred_element_type=jnp.float32)
+
+
+def dot_rows(left, right):
+    dims = (((1,), (1,)), ((), ()))
+    return lax.dot_general(left, right, dims, preferred_element_type=jnp.float32)
+
+
+def row_operand(value):
+    high, low = split(value)
+    return jnp.concatenate([high, high, low], axis=1)
 
 
 def flow_solver(
@@ -319,7 +325,11 @@
     partial,
     driven,
     images,
-    image,
+    ordered,
+    summed,
+    lefts,
+    products,
+    rights,
     out_fwd,
     in_fwd,
     out_back,
@@ -337,11 +347,11 @@
 ):
     group_size, minor, local_modes, rows, degrees, inner = sizes
     half = local_modes // 2
-    per_dot = 4
     me = lax.axis_index(AXES[0]) * minor + lax.axis_index(AXES[1])
     lane = lax.broadcasted_iota(jnp.int32, (1, LANES), 1)
-    first_half = lane % local_modes < half
+    even_lane = lane % 2 == 0
     low_flow = lane < local_modes
+    low_rows = lax.broadcasted_iota(jnp.int32, (8, LANES), 0) % 4 < 2
 
     def own_rows(index):
         return pl.ds(pl.multiple_of(index * rows, rows), rows)
@@ -378,104 +388,115 @@
         pltpu.make_async_copy(src, dst, recv_sem).wait()
 
     def to_modes(first, second):
-        turned = pltpu.roll(second, half, 1)
-        back = pltpu.roll(first, LANES - half, 1)
-        return jnp.where(first_half, first, turned), jnp.where(first_half, back, second)
+        turned = pltpu.roll(second, 1, 1)
+        back = pltpu.roll(first, LANES - 1, 1)
+        return jnp.where(even_lane, first, turned), jnp.where(even_lane, back, second)
+
+    def rows_of(field):
+        return dot_rows(to_rows_ref[...], row_operand(field.reshape(LANES, degrees)))
 
     def send_values(side, field):
-        values = dot(to_rows_ref[...], right_operand(field))
-        constant = jnp.logical_and(me + side == 0, lane % half == 0)
-        out_fwd[side] = values * jnp.where(constant, 0.5, 1.0)
+        constant = jnp.logical_and(me + side == 0, lane < 4)
+        out_fwd[side] = rows_of(field) * jnp.where(constant, 0.5, 1.0)
         exchange(out_fwd.at[side], in_fwd.at[side], fwd_send.at[side], fwd_recv.at[side])
 
-    def points_of_rows(pair):
-        columns = []
-        for row in (2 * pair, 2 * pair + 1):
-            picked = pl.ds(row, group_size, stride=rows)
-            real, imag = to_modes(in_fwd[0, picked, :], in_fwd[1, picked, :])
-            columns.append(jnp.concatenate([real, imag], axis=0))
-        operand = right_operand(jnp.concatenate(columns, axis=1))
-        summed = dot(gather_ref[...], operand)
+    pairs = range(rows // 2)
+
+    def sums_over_sources():
+        for pair in pairs:
+            columns = []
+            for row in (2 * pair, 2 * pair + 1):
+                picked = pl.ds(row, group_size, stride=rows)
+                real, imag = to_modes(in_fwd[0, picked, :], in_fwd[1, picked, :])
+                columns.append(jnp.concatenate([real, imag], axis=0))
+            operand = right_operand(jnp.concatenate(columns, axis=1))
+            summed[pair] = dot(gather_ref[...], operand)
         cos, sin, low = twist_ref[0], twist_ref[1], twist_ref[2]
-        lefts = []
-        for index in range(2):
-            part = summed[:, index * LANES : (index + 1) * LANES]
+        for row in range(rows):
+            pair, index = divmod(row, 2)
+            lanes = slice(index * LANES, (index + 1) * LANES)
             real, imag, wave_real, wave_imag = (
-                part[n * inner : (n + 1) * inner] for n in range(4)
+                summed[pair, n * inner : (n + 1) * inner, lanes] for n in range(4)
             )
             slope_real = -(wave_imag + low * imag)
             slope_imag = wave_real + low * real
-            for re, im in ((real, imag), (slope_real, slope_imag)):
+            for part, (re, im) in enumerate(((real, imag), (slope_real, slope_imag))):
                 re_high, re_low = split(re * cos - im * sin)
                 im_high, im_low = split(re * sin + im * cos)
-                lefts.append(jnp.concatenate([re_high, im_high, re_low, im_low], axis=1))
-        wide = dot(jnp.concatenate(lefts, axis=0), finish_ref[...])
+                where = slice((2 * part + index) * inner, (2 * part + index + 1) * inner)
+                lefts[pair, where] = jnp.concatenate([re_high, im_high, re_low, im_low], axis=1)
+
+    def points_of_rows(pair):
+        wide = dot(lefts[pair], finish_ref[...])
         points = wide[:, :LANES] + wide[:, LANES:]
-        for index in range(2):
-            where = pl.ds((2 * pair + index) * inner, inner)
-            image[0, where, :] = points[2 * index * inner : (2 * index + 1) * inner]
-            image[1, where, :] = points[(2 * index + 1) * inner : (2 * index + 2) * inner]
+        return points[: 2 * inner], points[2 * inner :]
 
     def receive_points():
         for side in range(2):
             finish_exchange(
                 out_fwd.at[side], in_fwd.at[side], fwd_send.at[side], fwd_recv.at[side]
             )
-        for pair in range(rows // 2):
-            points_of_rows(pair)
-
-    def modes_of_rows(pair, slot, factor):
-        where = pl.ds(2 * pair * inner, 2 * inner)
-        product = factor * (
-            images[0, 0, where, :] * images[slot, 1, where, :]
-            + images[slot, 0, where, :] * images[0, 1, where, :]
-        )
+        sums_over_sources()
+
+    def pair_rows(pair):
+        return pl.ds(2 * pair * inner, 2 * inner)
+
+    def keep_product(pair, product):
         high, low = split(product)
-        turned = dot(jnp.concatenate([high, low, high], axis=1), begin_ref[...])
+        products[pair] = jnp.concatenate([high, low, high], axis=1)
+
+    def send_products():
         cos, sin = twist_ref[0], twist_ref[1]
-        columns = []
-        for index in range(2):
-            part = turned[index * inner : (index + 1) * inner]
-            real, imag = part[:, :LANES], part[:, LANES:]
-            columns.append(
-                jnp.concatenate([real * cos + imag * sin, imag * cos - real * sin], axis=0)
-            )
-        operand = right_operand(jnp.concatenate(columns, axis=1))
-        summed = dot(scatter_ref[...], operand)
-        for index in range(2):
-            part = summed[:, index * LANES : (index + 1) * LANES]
-            first, second = to_modes(part[:group_size], part[group_size:])
-            picked = pl.ds(2 * pair + index, group_size, stride=rows)
-            out_back[0, picked, :] = first
-            out_back[1, picked, :] = second
-
-    def precondition(side, operand):
-        for block in range(half // per_dot):
-            base = side * half + block * per_dot
-            where = pl.ds(pl.multiple_of(base * degrees, degrees), per_dot * degrees)
-            wide = dot(tau_terms[where, :], operand)
-            narrow = wide[:, :LANES] + wide[:, LANES:]
-            total = applied[side]
-            for index in range(per_dot):
-                mine = lane % half == block * per_dot + index
-                total = jnp.where(mine, narrow[index * degrees : (index + 1) * degrees], total)
-            applied[side] = total
-
-    def by_flow(values, masks):
-        low = jnp.sum(jnp.where(jnp.logical_and(masks, low_flow), values, 0.0), axis=1, keepdims=True)
-        high = jnp.sum(
-            jnp.where(jnp.logical_and(masks, ~low_flow), values, 0.0), axis=1, keepdims=True
-        )
-        return jnp.where(low_flow, low, high)
+        for pair in pairs:
+            turned = dot(products[pair], begin_ref[...])
+            columns = []
+            for index in range(2):
+                part = turned[index * inner : (index + 1) * inner]
+                real, imag = part[:, :LANES], part[:, LANES:]
+                columns.append(
+                    jnp.concatenate([real * cos + imag * sin, imag * cos - real * sin], axis=0)
+                )
+            rights[pair] = right_operand(jnp.concatenate(columns, axis=1))
+        for pair in pairs:
+            spread = dot(scatter_ref[...], rights[pair])
+            for index in range(2):
+                part = spread[:, index * LANES : (index + 1) * LANES]
+                first, second = to_modes(part[:group_size], part[group_size:])
+                picked = pl.ds(2 * pair + index, group_size, stride=rows)
+                out_back[0, picked, :] = first
+                out_back[1, picked, :] = second
+        for side in range(2):
+            exchange(out_back.at[side], in_back.at[side], back_send.at[side], back_recv.at[side])
+
+    top_rows = lax.broadcasted_iota(jnp.int32, (8, degrees), 0) < 4
+
+    def precondition(side, field):
+        high = field.astype(jnp.bfloat16).astype(jnp.float32)
+        terms = [part.reshape(LANES // 8, 8, degrees) for part in (high, field - high)]
+        terms = jnp.stack(terms, axis=1).reshape(2 * LANES, degrees).astype(jnp.bfloat16)
+        for pair in range(half // 2):
+            left = terms[16 * pair : 16 * pair + 16]
+            left = jnp.concatenate([left, left], axis=1)
+            found = []
+            for index in range(2):
+                base = (side * half + 2 * pair + index) * 2 * degrees
+                where = pl.ds(pl.multiple_of(base, 2 * degrees), 2 * degrees)
+                both = dot(left, tau_terms[where, :])
+                found.append(both[:8] + both[8:])
+            applied[side, pair] = jnp.where(top_rows, found[0], found[1])
 
     stat_row = lax.broadcasted_iota(jnp.int32, (8, LANES), 0)
-    stat_lane = lax.broadcasted_iota(jnp.int32, (8, LANES), 1) % local_modes
-    packed = stat_row == stat_lane
-
-    def send_stats(partial):
-        sums = by_flow(partial, stat_row >= 0)
+    packed = stat_row == lax.broadcasted_iota(jnp.int32, (8, LANES), 1)
+
+    def send_stats():
+        sums = []
+        for chosen in (low_rows, ~low_rows):
+            for known in range(KRYLOV + 1):
+                sums.append(
+                    jnp.sum(jnp.where(chosen, partial[known], 0.0), axis=0, keepdims=True)
+                )
+        sums = jnp.sum(jnp.concatenate(sums, axis=0), axis=1, keepdims=True)
         out_stat[...] = jnp.sum(jnp.where(packed, sums, 0.0), axis=0, keepdims=True)
-
         for peer, place in peers():
             pltpu.make_async_remote_copy(
                 src_ref=out_stat,
@@ -492,52 +513,82 @@
         pltpu.make_async_copy(in_stat.at[sent], in_stat.at[sent], stat_send).wait()
         pltpu.make_async_copy(in_stat, in_stat, stat_recv).wait()
         total = jnp.sum(in_stat[...], axis=0)
-        return by_flow(jnp.broadcast_to(total, (8, LANES)), packed)
-
+        return jnp.sum(jnp.where(packed, total, 0.0), axis=1, keepdims=True)
+
+    def by_flow(stats, known):
+        low = jnp.broadcast_to(stats[known : known + 1], (8, LANES))
+        high = jnp.broadcast_to(stats[known + KRYLOV + 1 : known + KRYLOV + 2], (8, LANES))
+        return jnp.concatenate(
+            [jnp.where(low_flow, low, high), jnp.where(low_rows, low, high)], axis=0
+        )
+
+    def for_points(value):
+        return value[:1]
+
+    def for_coefs(value):
+        return jnp.concatenate([value[8:], value[8:]], axis=1)[None]
+
+    chunks, chunk = stage.shape[:2]
+
+    def fetch(index):
+        where = pl.ds(pl.multiple_of(index * chunk, chunk), chunk)
+        return pltpu.make_async_copy(taus_ref.at[where, :], stage.at[index], stage_sem.at[index])
+
+    def fetch_step(index, carry):
+        fetch(index).start()
+        return carry
+
+    lax.fori_loop(0, chunks, fetch_step, 0)
+
+    def spread_rows(field_ref):
+        for flow in range(2):
+            for part in range(2):
+                for side in range(2):
+                    rows_of_part = field_ref[flow, part, pl.ds(side * half, half), :]
+                    where = pl.ds(2 * flow + part, half, stride=4)
+                    for column in range(2):
+                        lanes = slice(column * LANES, (column + 1) * LANES)
+                        ordered[side, column, where, :] = rows_of_part[:, lanes]
+
+    def in_order(side):
+        return jnp.concatenate([ordered[side, 0], ordered[side, 1]], axis=1)
+
+    spread_rows(forcing_ref)
     vectors[...] = jnp.zeros_like(vectors)
     images[...] = jnp.zeros_like(images)
-    vectors[0] = start_ref[...]
     for side in range(2):
-        send_values(side, start_ref[side])
-        driven[side] = dot(to_rows_ref[...], right_operand(forcing_ref[side]))
-
-    chunk = stage.shape[1]
-    chunks = tau_terms.shape[0] // chunk
-
-    def fetch(index, slot):
-        where = pl.ds(pl.multiple_of(index * chunk, chunk), chunk)
-        return pltpu.make_async_copy(taus_ref.at[where, :], stage.at[slot], stage_sem.at[slot])
+        driven[side] = rows_of(in_order(side))
+    spread_rows(start_ref)
+    for side in range(2):
+        vectors[0, side] = in_order(side).reshape(LANES // 8, 8, degrees)
+    for side in range(2):
+        send_values(side, vectors[0, side])
 
     def load(index, carry):
-        slot = lax.rem(index, 2)
-
-        @pl.when(index + 1 < chunks)
-        def _():
-            fetch(index + 1, 1 - slot).start()
-
-        fetch(index, slot).wait()
-        high, low = split(stage[slot])
-        combined = dot(jnp.concatenate([high, low, high], axis=1), to_degrees_ref[...])
-        high, low = split(combined)
-        where = pl.ds(pl.multiple_of(index * chunk, chunk), chunk)
-        tau_terms[where, :degrees] = high
-        tau_terms[where, degrees:] = low
+        fetch(index).wait()
+        for mode in range(chunk // degrees):
+            operand = row_operand(stage[index, mode * degrees : (mode + 1) * degrees])
+            high, low = split(dot_rows(to_degrees_ref[...], operand))
+            base = (index * (chunk // degrees) + mode) * 2 * degrees
+            base = pl.multiple_of(base, 2 * degrees)
+            tau_terms[pl.ds(base, degrees), :] = high
+            tau_terms[pl.ds(base + degrees, degrees), :] = low
         return carry
 
-    fetch(0, 0).start()
     lax.fori_loop(0, chunks // 2, load, 0)
 
     receive_points()
-    images[0] = image[...]
+    for pair in pairs:
+        points = points_of_rows(pair)
+        for part in range(2):
+            images[0, part, pair_rows(pair), :] = points[part]
+        keep_product(pair, STRENGTH * points[0] * points[1])
+    send_products()
+    steps = NEWTON * (KRYLOV + 1)
 
     def iteration(index, carry):
         phase = lax.rem(index, KRYLOV + 1)
         opening = phase == 0
-        factor = jnp.where(opening, 0.5 * STRENGTH, STRENGTH)
-        for pair in range(rows // 2):
-            modes_of_rows(pair, phase, factor)
-        for side in range(2):
-            exchange(out_back.at[side], in_back.at[side], back_send.at[side], back_recv.at[side])
 
         @pl.when(index == 0)
         def _():
@@ -550,23 +601,21 @@
             finish_exchange(
                 out_back.at[side], in_back.at[side], back_send.at[side], back_recv.at[side]
             )
-            high, low = split(in_back[side] - drive * driven[side])
-            both = jnp.concatenate([high, low], axis=1)
-            precondition(side, jnp.concatenate([both, both], axis=0))
+            precondition(side, (in_back[side] - drive * driven[side]).T)
             whole = vectors[phase, side] + applied[side]
             applied[side] = whole
-            sums = [
-                jnp.sum(vectors[known + 1, side] * whole, axis=0, keepdims=True)
-                for known in range(KRYLOV)
-            ]
-            sums = [jnp.where(known < phase, sums[known], 0.0) for known in range(KRYLOV)]
-            sums.append(jnp.sum(whole * whole, axis=0, keepdims=True))
-            sums += [jnp.zeros((1, LANES), jnp.float32)] * (7 - KRYLOV)
-            partial[...] += jnp.concatenate(sums, axis=0)
+
+            def add_stat(known, other):
+                summed = jnp.sum(other * whole, axis=0)
+                partial[known] += summed[:, :LANES] + summed[:, LANES:]
+
+            for known in range(KRYLOV):
+                add_stat(known, vectors[known + 1, side])
+            add_stat(KRYLOV, whole)
 
             @pl.when(side == 1)
             def _():
-                send_stats(partial[...])
+                send_stats()
 
             @pl.when(phase < KRYLOV)
             def _():
@@ -576,53 +625,81 @@
 
         lax.fori_loop(0, 2, half_step, 0)
         stats = receive_stats()
-        history[phase] = stats
-        inner_products = [stats[known : known + 1] for known in range(KRYLOV)]
-        square = stats[KRYLOV : KRYLOV + 1]
+        inner_products = [
+            jnp.where(known < phase, by_flow(stats, known), 0.0) for known in range(KRYLOV)
+        ]
+        square = by_flow(stats, KRYLOV)
         for value in inner_products:
             square = square - value * value
-        scale = jnp.where(opening, -1.0, 1.0) / jnp.sqrt(square)
+        length = jnp.sqrt(square)
+        scale = jnp.where(opening, -1.0, 1.0) / length
+        for known in range(KRYLOV):
+            history[phase, known] = inner_products[known]
+        history[phase, KRYLOV] = length
 
         @pl.when(phase < KRYLOV)
         def _():
             for side in range(2):
                 whole = applied[side]
                 for known in range(KRYLOV):
-                    whole = whole - inner_products[known] * vectors[known + 1, side]
-                vectors[phase + 1, side] = scale * whole
+                    whole = whole - for_coefs(inner_products[known]) * vectors[known + 1, side]
+                vectors[phase + 1, side] = for_coefs(scale) * whole
             receive_points()
-            for part in range(2):
-                whole = image[part]
-                for known in range(KRYLOV):
-                    whole = whole - inner_products[known] * images[known + 1, part]
-                images[phase + 1, part] = scale * whole
+            for pair in pairs:
+                where = pair_rows(pair)
+                fresh = []
+                for part, whole in enumerate(points_of_rows(pair)):
+                    for known in range(KRYLOV):
+                        factor = for_points(inner_products[known])
+                        whole = whole - factor * images[known + 1, part, where, :]
+                    fresh.append(for_points(scale) * whole)
+                    images[phase + 1, part, where, :] = fresh[part]
+                crossed = images[0, 0, where, :] * fresh[1] + fresh[0] * images[0, 1, where, :]
+                keep_product(pair, STRENGTH * crossed)
+            send_products()
 
         @pl.when(phase == KRYLOV)
         def _():
-            hessen = []
+            matrix = []
             for column in range(KRYLOV):
-                kept = history[column + 1]
-                entries = [kept[known : known + 1] for known in range(column + 1)]
-                length = kept[KRYLOV : KRYLOV + 1]
-                for value in entries:
-                    length = length - value * value
-                hessen.append(jnp.stack(entries + [jnp.sqrt(length)], axis=1))
-            solved = least_squares(hessen, jnp.sqrt(history[0][KRYLOV : KRYLOV + 1]))
+                entries = [history[column + 1, known] for known in range(column + 1)]
+                matrix.append(entries + [history[column + 1, KRYLOV]])
+            solved = least_squares(matrix, history[0, KRYLOV])
             for side in range(2):
                 whole = vectors[0, side]
                 for known in range(KRYLOV):
-                    whole = whole + solved[known] * vectors[known + 1, side]
+                    whole = whole + for_coefs(solved[known]) * vectors[known + 1, side]
                 vectors[0, side] = whole
-            for part in range(2):
-                whole = images[0, part]
-                for known in range(KRYLOV):
-                    whole = whole + solved[known] * images[known + 1, part]
-                images[0, part] = whole
+
+            @pl.when(index + 1 < steps)
+            def _():
+                for pair in pairs:
+                    where = pair_rows(pair)
+                    fresh = []
+                    for part in range(2):
+                        whole = images[0, part, where, :]
+                        for known in range(KRYLOV):
+                            factor = for_points(solved[known])
+                            whole = whole + factor * images[known + 1, part, where, :]
+                        fresh.append(whole)
+                        images[0, part, where, :] = whole
+                    keep_product(pair, STRENGTH * fresh[0] * fresh[1])
+                send_products()
 
         return carry
 
-    lax.fori_loop(0, NEWTON * (KRYLOV + 1), iteration, 0)
-    out_ref[...] = vectors[0]
+    lax.fori_loop(0, steps, iteration, 0)
+    for side in range(2):
+        whole = vectors[0, side].reshape(LANES, degrees)
+        ordered[side, 0] = whole[:, :LANES]
+        ordered[side, 1] = whole[:, LANES:]
+    for flow in range(2):
+        for part in range(2):
+            for side in range(2):
+                where = pl.ds(2 * flow + part, half, stride=4)
+                out_ref[flow, part, pl.ds(side * half, half), :] = jnp.concatenate(
+                    [ordered[side, 0, where, :], ordered[side, 1, where, :]], axis=1
+                )
 
 
 def solve_flows(start, forcing, taus):
@@ -635,40 +712,39 @@
     tables = tables_of(local_modes, group_size, degrees)
     sizes = (group_size, minor, local_modes, rows, degrees, inner)
 
-    def pack(field):
-        field = field.reshape(batch, parts, 2, half, degrees)
-        return field.transpose(2, 4, 0, 1, 3).reshape(2, degrees, LANES)
-
-    def unpack(field):
-        field = field.reshape(2, degrees, batch, parts, half)
-        return field.transpose(2, 3, 0, 4, 1).reshape(batch, parts, local_modes, degrees)
+    coefs = (2, LANES // 8, 8, degrees)
 
     field = (2, degrees, LANES)
     image = (2, rows * inner, LANES)
     chunk = 4 * degrees
+    chunks = local_modes // 4
     vmem = pl.BlockSpec(memory_space=pltpu.VMEM)
     out = pl.pallas_call(
         functools.partial(flow_solver, sizes),
-        out_shape=jax.ShapeDtypeStruct(field, jnp.float32),
+        out_shape=jax.ShapeDtypeStruct(start.shape, jnp.float32),
         in_specs=[vmem, vmem, pl.BlockSpec(memory_space=pl.ANY)] + [vmem] * len(tables),
         out_specs=vmem,
         scratch_shapes=[
-            pltpu.VMEM((local_modes * degrees, 2 * degrees), jnp.bfloat16),
-            pltpu.VMEM((2, chunk, degrees), jnp.float32),
-            pltpu.VMEM((KRYLOV + 1,) + field, jnp.float32),
-            pltpu.VMEM(field, jnp.float32),
-            pltpu.VMEM((8, LANES), jnp.float32),
+            pltpu.VMEM((local_modes * 2 * degrees, degrees), jnp.bfloat16),
+            pltpu.VMEM((chunks, chunk, degrees), jnp.float32),
+            pltpu.VMEM((KRYLOV + 1,) + coefs, jnp.float32),
+            pltpu.VMEM(coefs, jnp.float32),
+            pltpu.VMEM((KRYLOV + 1, 8, LANES), jnp.float32),
             pltpu.VMEM(field, jnp.float32),
             pltpu.VMEM((KRYLOV + 1,) + image, jnp.float32),
-            pltpu.VMEM(image, jnp.float32),
+            pltpu.VMEM((2, 2, LANES, LANES), jnp.float32),
+            pltpu.VMEM((rows // 2, 4 * inner, 2 * LANES), jnp.float32),
+            pltpu.VMEM((rows // 2, 4 * inner, 4 * LANES), jnp.bfloat16),
+            pltpu.VMEM((rows // 2, 2 * inner, 3 * LANES), jnp.bfloat16),
+            pltpu.VMEM((rows // 2, 6 * inner, 2 * LANES), jnp.bfloat16),
             pltpu.VMEM(field, jnp.float32),
             pltpu.VMEM(field, jnp.float32),
             pltpu.VMEM(field, jnp.float32),
             pltpu.VMEM(field, jnp.float32),
             pltpu.VMEM((1, LANES), jnp.float32),
             pltpu.VMEM((group_size, 1, LANES), jnp.float32),
-            pltpu.VMEM((KRYLOV + 1, 8, LANES), jnp.float32),
-            pltpu.SemaphoreType.DMA((2,)),
+            pltpu.VMEM((KRYLOV + 1, KRYLOV + 1, 16, LANES), jnp.float32),
+            pltpu.SemaphoreType.DMA((chunks,)),
         ]
         + [pltpu.SemaphoreType.DMA((2,))] * 4
         + [pltpu.SemaphoreType.DMA] * 2,
@@ -676,12 +752,12 @@
             has_side_effects=True, vmem_limit_bytes=56 * 1024 * 1024
         ),
     )(
-        pack(start),
-        pack(forcing),
+        start,
+        forcing,
         taus.reshape(local_modes * degrees, degrees),
         *[jnp.asarray(table) for table in tables],
     )
-    return unpack(out)
+    return out
 
 
 def fits_kernel(start):

time: 183 us -> 157 us (0.86)
  Pallas kernels: 177 us -> 155 us
  local copies, waits for them, and re-layouts: 5.4 us -> 1.67 us
    pallas_call x1, Pallas kernels: 177 us -> 155 us  [solve_flows(): pl.pallas_call(functools.partial(flow_solver, sizes), out_shape=jax.Shape...]
    transpose x3 -> x0, local copies, waits for them, and re-layouts: 2.66 us -> none  [the longest x2 1.93 us: pack(): return field.transpose(2, 4, 0, 1, 3).reshape(2, degrees, LANES)]
where the time goes in v2:
time: 157 us; the launch traced here: 156 us
  Pallas kernels  155 us (99%)
  local copies, waits for them, and re-layouts  1.67 us (1%)
    pallas_call x1, Pallas kernels, solve_flows(): pl.pallas_call(functools.partial(flow_solver, sizes), out_shape=jax.Shape...  155 us

profile of v2, /device:TPU:0, one launch (start us, length us, event | category | flops | bytes accessed | tf_op | source)
XLA Modules:
  0.0 156.4 jit_solution(16943779806342683815)
XLA Ops:
  0.0 154.7 %shard_map.100 = f32[2,2,64,256]{3,2,1,0:T(8,128)} custom-call(f32[2,2,64,256]{3,2,1,0:T(8,128)} %start_ref.1, f32[2,2,64,256]{3,2,1,0:T(8,128)} %forcing_ref.1, f32[16384,256]{1,0:T(8,128)} %bitcast.1, bf16[256,768]{1,0:T(8,128)(2,1)} %constant.14.clone.to_rows_ref, bf16[256,768]{1,0:T(8,128)(2,1)} %constant.15.clone.to_degrees_ref, ...), custom_call_target="tpu_custom_call" | custom-call | tf_op jit(solution)/shard_map/pallas_call | solution.py:722
  154.7 1.7 %copy.12 = f32[2,2,64,256]{3,2,1,0:T(8,128)} copy(f32[2,2,64,256]{3,2,1,0:T(8,128)} %shard_map.100) | data formatting | bytes 524288

commit v3 on v2

--- a/solution.py
+++ b/solution.py
@@ -310,6 +310,14 @@
     start_ref,
     forcing_ref,
     taus_ref,
+    to_rows_hbm,
+    to_degrees_hbm,
+    gather_hbm,
+    scatter_hbm,
+    twist_hbm,
+    finish_hbm,
+    begin_hbm,
+    out_ref,
     to_rows_ref,
     to_degrees_ref,
     gather_ref,
@@ -317,7 +325,6 @@
     twist_ref,
     finish_ref,
     begin_ref,
-    out_ref,
     tau_terms,
     stage,
     vectors,
@@ -338,6 +345,7 @@
     in_stat,
     history,
     stage_sem,
+    table_sem,
     fwd_send,
     fwd_recv,
     back_send,
@@ -538,6 +546,26 @@
         fetch(index).start()
         return carry
 
+    barrier = pltpu.get_barrier_semaphore()
+    for _, place in peers():
+        pl.semaphore_signal(
+            barrier, inc=1, device_id=place, device_id_type=pl.DeviceIdType.MESH
+        )
+    tables = (
+        (to_rows_hbm, to_rows_ref),
+        (to_degrees_hbm, to_degrees_ref),
+        (gather_hbm, gather_ref),
+        (scatter_hbm, scatter_ref),
+        (twist_hbm, twist_ref),
+        (finish_hbm, finish_ref),
+        (begin_hbm, begin_ref),
+    )
+    tables = [
+        pltpu.make_async_copy(src, dst, table_sem.at[index])
+        for index, (src, dst) in enumerate(tables)
+    ]
+    for copy in tables:
+        copy.start()
     lax.fori_loop(0, chunks, fetch_step, 0)
 
     def spread_rows(field_ref):
@@ -553,16 +581,19 @@
     def in_order(side):
         return jnp.concatenate([ordered[side, 0], ordered[side, 1]], axis=1)
 
-    spread_rows(forcing_ref)
     vectors[...] = jnp.zeros_like(vectors)
     images[...] = jnp.zeros_like(images)
-    for side in range(2):
-        driven[side] = rows_of(in_order(side))
     spread_rows(start_ref)
+    for copy in tables:
+        copy.wait()
+    pl.semaphore_wait(barrier, group_size - 1)
     for side in range(2):
         vectors[0, side] = in_order(side).reshape(LANES // 8, 8, degrees)
     for side in range(2):
         send_values(side, vectors[0, side])
+    spread_rows(forcing_ref)
+    for side in range(2):
+        driven[side] = rows_of(in_order(side))
 
     def load(index, carry):
         fetch(index).wait()
@@ -665,12 +696,6 @@
                 entries = [history[column + 1, known] for known in range(column + 1)]
                 matrix.append(entries + [history[column + 1, KRYLOV]])
             solved = least_squares(matrix, history[0, KRYLOV])
-            for side in range(2):
-                whole = vectors[0, side]
-                for known in range(KRYLOV):
-                    whole = whole + for_coefs(solved[known]) * vectors[known + 1, side]
-                vectors[0, side] = whole
-
             @pl.when(index + 1 < steps)
             def _():
                 for pair in pairs:
@@ -686,6 +711,12 @@
                     keep_product(pair, STRENGTH * fresh[0] * fresh[1])
                 send_products()
 
+            for side in range(2):
+                whole = vectors[0, side]
+                for known in range(KRYLOV):
+                    whole = whole + for_coefs(solved[known]) * vectors[known + 1, side]
+                vectors[0, side] = whole
+
         return carry
 
     lax.fori_loop(0, steps, iteration, 0)
@@ -722,9 +753,10 @@
     out = pl.pallas_call(
         functools.partial(flow_solver, sizes),
         out_shape=jax.ShapeDtypeStruct(start.shape, jnp.float32),
-        in_specs=[vmem, vmem, pl.BlockSpec(memory_space=pl.ANY)] + [vmem] * len(tables),
+        in_specs=[vmem, vmem] + [pl.BlockSpec(memory_space=pl.ANY)] * (1 + len(tables)),
         out_specs=vmem,
-        scratch_shapes=[
+        scratch_shapes=[pltpu.VMEM(table.shape, table.dtype) for table in tables]
+        + [
             pltpu.VMEM((local_modes * 2 * degrees, degrees), jnp.bfloat16),
             pltpu.VMEM((chunks, chunk, degrees), jnp.float32),
             pltpu.VMEM((KRYLOV + 1,) + coefs, jnp.float32),
@@ -745,11 +777,12 @@
             pltpu.VMEM((group_size, 1, LANES), jnp.float32),
             pltpu.VMEM((KRYLOV + 1, KRYLOV + 1, 16, LANES), jnp.float32),
             pltpu.SemaphoreType.DMA((chunks,)),
+            pltpu.SemaphoreType.DMA((len(tables),)),
         ]
         + [pltpu.SemaphoreType.DMA((2,))] * 4
         + [pltpu.SemaphoreType.DMA] * 2,
         compiler_params=pltpu.CompilerParams(
-            has_side_effects=True, vmem_limit_bytes=56 * 1024 * 1024
+            collective_id=0, has_side_effects=True, vmem_limit_bytes=56 * 1024 * 1024
         ),
     )(
         start,

time: 157 us -> 153 us (0.975)
  Pallas kernels: 155 us -> 151 us
    pallas_call x1, Pallas kernels: 155 us -> 151 us  [solve_flows(): pl.pallas_call(functools.partial(flow_solver, sizes), out_shape=jax.Shape...]
where the time goes in v3:
time: 153 us
  Pallas kernels  151 us (99%)
  local copies, waits for them, and re-layouts  1.67 us (1%)
    pallas_call x1, Pallas kernels, solve_flows(): pl.pallas_call(functools.partial(flow_solver, sizes), out_shape=jax.Shape...  151 us

profile of v3, /device:TPU:0, one launch (start us, length us, event | category | flops | bytes accessed | tf_op | source)
XLA Modules:
  0.0 152.6 jit_solution(779096826382680950)
XLA Ops:
  0.0 151.0 %shard_map.100 = f32[2,2,64,256]{3,2,1,0:T(8,128)} custom-call(f32[2,2,64,256]{3,2,1,0:T(8,128)} %start_ref.1, f32[2,2,64,256]{3,2,1,0:T(8,128)} %forcing_ref.1, f32[16384,256]{1,0:T(8,128)} %bitcast.1, bf16[256,768]{1,0:T(8,128)(2,1)} %constant.14.clone.to_rows_hbm, bf16[256,768]{1,0:T(8,128)(2,1)} %constant.15.clone.to_degrees_hbm, ...), custom_call_target="tpu_custom_call" | custom-call | tf_op jit(solution)/shard_map/pallas_call | solution.py:753
  151.0 1.7 %copy.12 = f32[2,2,64,256]{3,2,1,0:T(8,128)} copy(f32[2,2,64,256]{3,2,1,0:T(8,128)} %shard_map.100) | data formatting | bytes 524288

commit v4 on v3

--- a/solution.py
+++ b/solution.py
@@ -636,6 +636,10 @@
             whole = vectors[phase, side] + applied[side]
             applied[side] = whole
 
+            @pl.when(phase < KRYLOV)
+            def _():
+                send_values(side, applied[side])
+
             def add_stat(known, other):
                 summed = jnp.sum(other * whole, axis=0)
                 partial[known] += summed[:, :LANES] + summed[:, LANES:]
@@ -648,13 +652,13 @@
             def _():
                 send_stats()
 
-            @pl.when(phase < KRYLOV)
-            def _():
-                send_values(side, applied[side])
-
             return carry
 
         lax.fori_loop(0, 2, half_step, 0)
+        @pl.when(phase < KRYLOV)
+        def _():
+            receive_points()
+
         stats = receive_stats()
         inner_products = [
             jnp.where(known < phase, by_flow(stats, known), 0.0) for known in range(KRYLOV)
@@ -670,12 +674,6 @@
 
         @pl.when(phase < KRYLOV)
         def _():
-            for side in range(2):
-                whole = applied[side]
-                for known in range(KRYLOV):
-                    whole = whole - for_coefs(inner_products[known]) * vectors[known + 1, side]
-                vectors[phase + 1, side] = for_coefs(scale) * whole
-            receive_points()
             for pair in pairs:
                 where = pair_rows(pair)
                 fresh = []
@@ -688,6 +686,11 @@
                 crossed = images[0, 0, where, :] * fresh[1] + fresh[0] * images[0, 1, where, :]
                 keep_product(pair, STRENGTH * crossed)
             send_products()
+            for side in range(2):
+                whole = applied[side]
+                for known in range(KRYLOV):
+                    whole = whole - for_coefs(inner_products[known]) * vectors[known + 1, side]
+                vectors[phase + 1, side] = for_coefs(scale) * whole
 
         @pl.when(phase == KRYLOV)
         def _():

time: 153 us -> 155 us (1.013)
  Pallas kernels: 151 us -> 153 us
    pallas_call x1, Pallas kernels: 151 us -> 153 us  [solve_flows(): pl.pallas_call(functools.partial(flow_solver, sizes), out_shape=jax.Shape...]
where the time goes in v4:
time: 155 us
  Pallas kernels  153 us (99%)
  local copies, waits for them, and re-layouts  1.67 us (1%)
    pallas_call x1, Pallas kernels, solve_flows(): pl.pallas_call(functools.partial(flow_solver, sizes), out_shape=jax.Shape...  153 us

profile of v4, /device:TPU:0, one launch (start us, length us, event | category | flops | bytes accessed | tf_op | source)
XLA Modules:
  0.0 154.9 jit_solution(6764952375413374296)
XLA Ops:
  0.0 153.2 %shard_map.100 = f32[2,2,64,256]{3,2,1,0:T(8,128)} custom-call(f32[2,2,64,256]{3,2,1,0:T(8,128)} %start_ref.1, f32[2,2,64,256]{3,2,1,0:T(8,128)} %forcing_ref.1, f32[16384,256]{1,0:T(8,128)} %bitcast.1, bf16[256,768]{1,0:T(8,128)(2,1)} %constant.14.clone.to_rows_hbm, bf16[256,768]{1,0:T(8,128)(2,1)} %constant.15.clone.to_degrees_hbm, ...), custom_call_target="tpu_custom_call" | custom-call | tf_op jit(solution)/shard_map/pallas_call | solution.py:756
  153.2 1.7 %copy.12 = f32[2,2,64,256]{3,2,1,0:T(8,128)} copy(f32[2,2,64,256]{3,2,1,0:T(8,128)} %shard_map.100) | data formatting | bytes 524288
